TPU v7x, 32 devices: a whole 2x2x4 slice. The times are simulated.
32 devices in a mesh: dp: 4 (over x, core), half: 2 (over y), own: 4 (over z).
Axes of the slice: x: 2, y: 2, z: 4, core: 2. Of those that a mesh axis runs over, the one named last changes fastest.
Arguments:
- grad_parts: bfloat16 [4, 6, 1024, 1024], P('dp', None, ('half', 'own')), may hold values from -6 to 6
- owner_table: int32 [6, 1], replicated, may hold values from 0 to 3; in each aligned block of 6 rows (0 to 5, 6 to 11, ...) at most 2 rows name the same one
- left_basis: bfloat16 [8, 1024, 1024], P(('half', 'own')), may hold values from -0.1875 to 0.1875
- right_basis: bfloat16 [8, 1024, 1024], P(('half', 'own')), may hold values from -0.1875 to 0.1875
- first_moment: bfloat16 [8, 1024, 1024], P(('half', 'own'), 'dp'), may hold values from -6 to 6
- second_moment: bfloat16 [8, 1024, 1024], P(('half', 'own'), 'dp'), may hold values from 0.5 to 8
Outputs:
- update: bfloat16 [6, 1024, 1024], P(None, ('half', 'own'), 'dp')
Inputs may be any that keep to these rules, and one draw needn't show every extreme that they name: `owner_table`: every owner index is named by at least one block and by at most 2 blocks; some owner is named by exactly 2 blocks.
All inputs are finite; a program needn't handle non-finite values.
Results may differ from a plain program's by a relative error of at most 0.013.
Values may be sent and summed in bfloat16 or wider, within the bound.
A program may use at most 128 MiB of HBM per device.

v0:
```python
import jax
import jax.numpy as jnp
from jax import lax
from jax.sharding import PartitionSpec as P

beta_first = 0.9
beta_second = 0.95
bias_first = 1.0 - 0.9**10
bias_second = 1.0 - 0.95**10
epsilon = 1e-08


def slot_select(owner_table, owner_count, slot_count):
    owner_ids = owner_table[:, 0]
    positions = jnp.arange(owner_ids.shape[0], dtype=jnp.int32)
    shared = (owner_ids[:, None] == owner_ids[None, :]) & (positions[None, :] < positions[:, None])
    ranking = jnp.sum(shared.astype(jnp.int32), axis=1)
    slot_ids = ranking * owner_count + owner_ids
    slot_range = jnp.arange(slot_count, dtype=jnp.int32)
    return (slot_range[:, None] == slot_ids[None, :]).astype(jnp.bfloat16)


def local(grad_parts, owner_table, left_basis, right_basis, first_moment, second_moment):
    halves = lax.axis_size("half")
    owners = lax.axis_size("own")
    replicas = lax.axis_size("dp")
    block_count = grad_parts.shape[1]
    piece_rows = grad_parts.shape[2]
    block_width = grad_parts.shape[3]
    quarter = block_width // replicas
    offset = lax.axis_index("dp") * quarter
    summed = lax.psum_scatter(
        grad_parts[0].astype(jnp.float32).astype(jnp.bfloat16),
        "dp",
        scatter_dimension=2,
        tiled=True,
    )
    selector = slot_select(owner_table, owners, halves * owners)
    flat_grad = summed.reshape(block_count, piece_rows * quarter)
    packed = jnp.dot(selector, flat_grad, preferred_element_type=jnp.float32).astype(jnp.bfloat16)
    packed = packed.reshape(halves, owners, piece_rows, quarter)
    arrived = lax.all_to_all(
        lax.all_to_all(packed, "half", split_axis=0, concat_axis=0, tiled=True),
        "own",
        split_axis=1,
        concat_axis=1,
        tiled=True,
    )
    grad_block = arrived.reshape(block_width, quarter)
    left_matrix = left_basis[0]
    right_matrix = right_basis[0]
    right_rows = lax.dynamic_slice_in_dim(right_matrix, offset, quarter, 0)
    left_slice = lax.dynamic_slice_in_dim(left_matrix, offset, quarter, 1)
    projected = lax.dot_general(
        left_slice,
        lax.all_gather(grad_block, "dp", axis=1, tiled=True),
        (((0,), (0,)), ((), ())),
        preferred_element_type=jnp.float32,
    )
    rotated = jnp.dot(
        projected.astype(jnp.bfloat16), right_matrix, preferred_element_type=jnp.float32
    )
    first_new = beta_first * first_moment[0].astype(jnp.float32) + (1.0 - beta_first) * rotated
    second_new = (
        beta_second * second_moment[0].astype(jnp.float32) + (1.0 - beta_second) * rotated * rotated
    )
    direction = (first_new / bias_first / (jnp.sqrt(second_new / bias_second) + epsilon)).astype(
        jnp.bfloat16
    )
    partial_cols = lax.dot_general(
        lax.all_gather(direction, "dp", axis=0, tiled=True),
        right_rows,
        (((1,), (1,)), ((), ())),
        preferred_element_type=jnp.float32,
    )
    update_block = jnp.dot(
        left_matrix, partial_cols.astype(jnp.bfloat16), preferred_element_type=jnp.float32
    )
    outgoing = update_block.astype(jnp.bfloat16).reshape(halves, owners, piece_rows, quarter)
    returned = lax.all_to_all(
        lax.all_to_all(outgoing, "half", split_axis=0, concat_axis=0, tiled=True),
        "own",
        split_axis=1,
        concat_axis=1,
        tiled=True,
    )
    flat_back = returned.reshape(halves * owners, piece_rows * quarter)
    placed = lax.dot_general(
        selector, flat_back, (((0,), (0,)), ((), ())), preferred_element_type=jnp.float32
    )
    return placed.astype(jnp.bfloat16).reshape(block_count, piece_rows, quarter)


def solution(mesh):
    return jax.shard_map(
        local,
        mesh=mesh,
        in_specs=(
            P("dp", None, ("half", "own"), None),
            P(),
            P(("half", "own"), None, None),
            P(("half", "own"), None, None),
            P(("half", "own"), "dp", None),
            P(("half", "own"), "dp", None),
        ),
        out_specs=P(None, ("half", "own"), "dp"),
        check_vma=False,
    )
```

profile of v0, /device:TPU:0, one launch (start us, length us, event | category | flops | bytes accessed | tf_op | source)
XLA Modules:
  0.0 161.1 jit_solution(16821739264425904918)
XLA Ops:
  6.5 0.7 reduce-scatter.2.cloned.1.call-update
  7.3 0.0 all-gather.3.cloned.1.call-start
  7.3 0.9 convert_reduce_fusion
  8.2 0.7 multiply_add_fusion
  8.9 31.8 %reduce-scatter.2.cloned.1.call-done = bf16[6,128,256]{2,1,0:T(8,128)(2,1)} async-done(((bf16[6,128,1024]{2,1,0:T(8,128)(2,1)}), bf16[6,128,256]{2,1,0:T(8,128)(2,1)}) %reduce-scatter.2.cloned.1.call-update) | async-done | bytes 393232 | tf_op jit(solution)/shard_map/reduce_scatter | solution.py:32
  40.7 1.2 copy.26
  41.9 0.3 convolution_convert_fusion.1
  42.2 0.1 copy.27
  42.3 10.5 %all_to_all.20 = bf16[2,4,128,256]{3,2,1,0:T(8,128)(2,1)S(1)} all-to-all(bf16[2,4,128,256]{3,2,1,0:T(8,128)(2,1)S(1)} %bitcast.60), channel_id=1, replica_groups=mesh['dp'=4,'half'=2,'own'=4] {'half'}, dimensions={0} | all-to-all | bytes 1048576 | tf_op jit(solution)/shard_map/all_to_all | solution.py:43
  52.8 17.9 %all_to_all.21 = bf16[2,4,128,256]{3,2,0,1:T(8,128)(2,1)S(1)} all-to-all(bf16[2,4,128,256]{3,2,0,1:T(8,128)(2,1)S(1)} %copy.20), channel_id=1, replica_groups=mesh['dp'=4,'half'=2,'own'=4] {'own'}, dimensions={1} | all-to-all | bytes 1048576 | tf_op jit(solution)/shard_map/all_to_all | solution.py:42
  70.7 0.8 copy.21
  71.6 0.0 all-gather.3.cloned.1.call-update
  71.6 0.0 all-gather.5.cloned.1.call-start
  71.6 20.2 %all-gather.3.cloned.1.call-done = bf16[1024,1024]{1,0:T(8,128)(2,1)} async-done(((bf16[1024,256]{1,0:T(8,128)(2,1)}), bf16[1024,1024]{1,0:T(8,128)(2,1)}) %all-gather.3.cloned.1.call-update) | async-done | bytes 2097168 | tf_op jit(solution)/shard_map/all_gather | solution.py:56
  91.8 5.0 %fusion.16 = bf16[256,1024]{1,0:T(8,128)(2,1)} fusion(bf16[1,256,1024]{2,1,0:T(8,128)(2,1)S(1)} %copy-done.1, bf16[1,256,1024]{2,1,0:T(8,128)(2,1)S(1)} %copy-done.2, bf16[1,1024,1024]{2,1,0:T(8,128)(2,1)} %param.9, bf16[1024,1024]{1,0:T(8,128)(2,1)} %all-gather.3.cloned.1.call-done, bf16[1,1024,1024]{2,1,0:T(8,128)(2,1)S(1)} %copy-done, s32[]{:T(128)S(6)} %select_n.4), kind=kOutput, calls=%fused_computation.18 | convolution fusion | flops 1077673984 | bytes 6291460 | tf_op jit(solution)/shard_map/dot_general | solution.py:60
  96.8 0.0 all-gather.5.cloned.1.call-update
  96.8 22.7 %all-gather.5.cloned.1.call-done = bf16[1024,1024]{1,0:T(8,128)(2,1)} async-done(((bf16[256,1024]{1,0:T(8,128)(2,1)}), bf16[1024,1024]{1,0:T(8,128)(2,1)}) %all-gather.5.cloned.1.call-update) | async-done | bytes 2097168 | tf_op jit(solution)/shard_map/all_gather | solution.py:71
  119.5 4.0 %fusion.7 = bf16[1024,256]{0,1:T(8,128)(2,1)S(1)} fusion(bf16[1,1024,1024]{2,1,0:T(8,128)(2,1)S(1)} %copy-done, bf16[1024,1024]{1,0:T(8,128)(2,1)} %all-gather.5.cloned.1.call-done, bf16[1,1024,1024]{2,1,0:T(8,128)(2,1)} %param.9, s32[]{:T(128)S(6)} %select_n.4), kind=kOutput, calls=%fused_computation.10 | convolution fusion | flops 1074266112 | bytes 5242884 | tf_op jit(solution)/shard_map/dot_general | solution.py:76
  123.5 0.2 copy.25
  123.7 11.1 %all_to_all.22 = bf16[2,4,128,256]{3,2,1,0:T(8,128)(2,1)S(1)} all-to-all(bf16[2,4,128,256]{3,2,1,0:T(8,128)(2,1)S(1)} %bitcast.61), channel_id=1, replica_groups=mesh['dp'=4,'half'=2,'own'=4] {'half'}, dimensions={0} | all-to-all | bytes 1048576 | tf_op jit(solution)/shard_map/all_to_all | solution.py:81
  134.8 18.3 %all_to_all.23 = bf16[2,4,128,256]{3,2,0,1:T(8,128)(2,1)S(1)} all-to-all(bf16[2,4,128,256]{3,2,0,1:T(8,128)(2,1)S(1)} %copy.23), channel_id=1, replica_groups=mesh['dp'=4,'half'=2,'own'=4] {'own'}, dimensions={1} | all-to-all | bytes 1048576 | tf_op jit(solution)/shard_map/all_to_all | solution.py:80
  153.1 0.3 copy.28
  153.4 0.4 convolution_convert_fusion
  153.8 0.8 copy.31
  (10 shorter events, 0.1 us)
Async XLA Ops:
  6.5 85.3 %copy-start = (bf16[1,1024,1024]{2,1,0:T(8,128)(2,1)S(1)}, bf16[1,1024,1024]{2,1,0:T(8,128)(2,1)}, u32[]{:S(2)}) copy-start(bf16[1,1024,1024]{2,1,0:T(8,128)(2,1)} %param.8) | copy-start | bytes 6291460
  6.5 34.1 %reduce-scatter.2.cloned.1.call-start = ((), (), s32[]{:S(2)}) async-start(), calls=%async_computation.5 | async-start | bytes 1966080 | tf_op jit(solution)/shard_map/reduce_scatter | solution.py:32
  7.3 84.6 %all-gather.3.cloned.1.call-start = ((), (), s32[]{:S(2)}) async-start(), calls=%async_computation.6 | async-start | bytes 2621440 | tf_op jit(solution)/shard_map/all_gather | solution.py:56
  52.8 39.0 %copy-start.1 = (bf16[1,256,1024]{2,1,0:T(8,128)(2,1)S(1)}, bf16[1,256,1024]{2,1,0:T(8,128)(2,1)}, u32[]{:S(2)}) copy-start(bf16[1,256,1024]{2,1,0:T(8,128)(2,1)} %param.11) | copy-start | bytes 1572868
  52.8 39.0 %copy-start.2 = (bf16[1,256,1024]{2,1,0:T(8,128)(2,1)S(1)}, bf16[1,256,1024]{2,1,0:T(8,128)(2,1)}, u32[]{:S(2)}) copy-start(bf16[1,256,1024]{2,1,0:T(8,128)(2,1)} %param.10) | copy-start | bytes 1572868
  71.6 47.9 %all-gather.5.cloned.1.call-start = ((), (), s32[]{:S(2)}) async-start(), calls=%async_computation.7 | async-start | bytes 2621440 | tf_op jit(solution)/shard_map/all_gather | solution.py:71
Sparse Core Ops, SparseCore 0:
  9.9 30.7 reduce-scatter.1
  71.7 20.0 all-gather.2
  96.9 22.5 all-gather.4
where the time goes:
time: 162 us; the launch traced here: 161 us
  waiting for transfers between devices  75.4 us (47%)
  blocking collectives  57.7 us (36%)
  between operations  13.2 us (8%)
  matrix products  9.55 us (6%)
  local copies, waits for them, and re-layouts  3.59 us (2%)
    reduce_scatter x1, waiting for transfers between devices, local(): lax.psum_scatter(grad_parts[0].astype(jnp.float32).astype(jnp.bfloat16),...  31.8 us
    all_gather x1, waiting for transfers between devices, local(): lax.all_gather(direction, 'dp', axis=0, tiled=True)  22.7 us
    all_gather x1, waiting for transfers between devices, local(): lax.all_gather(grad_block, 'dp', axis=1, tiled=True)  20.2 us
    all_to_all x1, blocking collectives, local(): lax.all_to_all(lax.all_to_all(outgoing, 'half', split_axis=0, concat_axis...  18.3 us
    all_to_all x1, blocking collectives, local(): lax.all_to_all(lax.all_to_all(packed, 'half', split_axis=0, concat_axis=0...  17.9 us
    all_to_all x1, blocking collectives, local(): lax.all_to_all(outgoing, 'half', split_axis=0, concat_axis=0, tiled=True)  11.1 us
    all_to_all x1, blocking collectives, local(): lax.all_to_all(packed, 'half', split_axis=0, concat_axis=0, tiled=True)  10.5 us
    dot_general x1, matrix products, local(): jnp.dot(projected.astype(jnp.bfloat16), right_matrix, preferred_element_t...  4.95 us
  transfers between devices with their start and end apart: 3, of which 3 were waited for; matrix products, arithmetic and copies ran while one was open for 1% of the time, Pallas kernels for 0%

commit v1 on v0

--- a/solution.py
+++ b/solution.py
@@ -8,6 +8,19 @@
 bias_first = 1.0 - 0.9**10
 bias_second = 1.0 - 0.95**10
 epsilon = 1e-08
+
+
+def ring_gather(array, axis, dim):
+    ways = lax.axis_size(axis)
+    up = [(d, (d + 1) % ways) for d in range(ways)]
+    down = [(d, (d - 1) % ways) for d in range(ways)]
+    earlier, later = ([array], [array])
+    for _ in range(ways // 2):
+        earlier.append(lax.ppermute(earlier[-1], axis, up))
+    for _ in range((ways - 1) // 2):
+        later.append(lax.ppermute(later[-1], axis, down))
+    line = jnp.concatenate([*earlier[::-1], *later[1:]], axis=dim)
+    return jnp.roll(line, (lax.axis_index(axis) - ways // 2) * array.shape[dim], axis=dim)
 
 
 def slot_select(owner_table, owner_count, slot_count):
@@ -68,7 +81,7 @@
         jnp.bfloat16
     )
     partial_cols = lax.dot_general(
-        lax.all_gather(direction, "dp", axis=0, tiled=True),
+        ring_gather(direction, "dp", 0),
         right_rows,
         (((1,), (1,)), ((), ())),
         preferred_element_type=jnp.float32,

time: 162 us -> 167 us (1.031)
  local copies, waits for them, and re-layouts: 3.59 us -> 14.4 us
  blocking collectives: 57.7 us -> 52.1 us
  waiting for transfers between devices: 75.4 us -> 73 us
  starting transfers between devices: 0.08 us -> 2.09 us
    all_gather x1 -> x0, waiting for transfers between devices: 22.7 us -> none  [local(): lax.all_gather(direction, 'dp', axis=0, tiled=True)]
    ppermute x0 -> x3, waiting for transfers between devices: none -> 20.3 us  [the longest x2 20.3 us: ring_gather(): earlier.append(lax.ppermute(earlier[-1], axis, up))]
    unnamed x10 -> x15, local copies, waits for them, and re-layouts: 2.45 us -> 11.4 us
    all_to_all x1, blocking collectives: 18.3 us -> 14.9 us  [local(): lax.all_to_all(lax.all_to_all(outgoing, 'half', split_axis=0, concat_axis...]
    all_to_all x1, blocking collectives: 11.1 us -> 8.99 us  [local(): lax.all_to_all(outgoing, 'half', split_axis=0, concat_axis=0, tiled=True)]
    ppermute x0 -> x3, starting transfers between devices: none -> 2.05 us  [the longest x1 1.74 us: ring_gather(): later.append(lax.ppermute(later[-1], axis, down))]
    concatenate x0 -> x1, local copies, waits for them, and re-layouts: none -> 1.87 us  [ring_gather(): jnp.roll(line, (lax.axis_index(axis) - ways // 2) * array.shape[dim], axi...]
  transfers between devices with their start and end apart: 3 -> 5, of which waited for: 3 -> 4; matrix products, arithmetic and copies ran while one was open for 1% -> 3% of each run, Pallas kernels for 0% -> 0%
where the time goes in v1:
time: 167 us; the launch traced here: 165 us
  waiting for transfers between devices  73 us (44%)
  blocking collectives  52.1 us (31%)
  local copies, waits for them, and re-layouts  14.4 us (9%)
  between operations  13.5 us (8%)
  matrix products  8.83 us (5%)
  starting transfers between devices  2.09 us (1%)
    reduce_scatter x1, waiting for transfers between devices, local(): lax.psum_scatter(grad_parts[0].astype(jnp.float32).astype(jnp.bfloat16),...  31.8 us
    ppermute x2, waiting for transfers between devices, ring_gather(): earlier.append(lax.ppermute(earlier[-1], axis, up))  20.3 us
    all_gather x1, waiting for transfers between devices, local(): lax.all_gather(grad_block, 'dp', axis=1, tiled=True)  20.2 us
    all_to_all x1, blocking collectives, local(): lax.all_to_all(lax.all_to_all(packed, 'half', split_axis=0, concat_axis=0...  17.7 us
    all_to_all x1, blocking collectives, local(): lax.all_to_all(lax.all_to_all(outgoing, 'half', split_axis=0, concat_axis...  14.9 us
    unnamed x15, local copies, waits for them, and re-layouts  11.4 us
    all_to_all x1, blocking collectives, local(): lax.all_to_all(packed, 'half', split_axis=0, concat_axis=0, tiled=True)  10.5 us
    all_to_all x1, blocking collectives, local(): lax.all_to_all(outgoing, 'half', split_axis=0, concat_axis=0, tiled=True)  8.99 us
  transfers between devices with their start and end apart: 5, of which 4 were waited for; matrix products, arithmetic and copies ran while one was open for 3% of the time, Pallas kernels for 0%

profile of v1, /device:TPU:0, one launch (start us, length us, event | category | flops | bytes accessed | tf_op | source)
XLA Modules:
  0.0 165.5 jit_solution(10139168291565246528)
XLA Ops:
  6.5 0.7 reduce-scatter.2.cloned.1.call-update
  7.3 0.9 convert_reduce_fusion
  8.9 31.8 %reduce-scatter.2.cloned.1.call-done = bf16[6,128,256]{2,1,0:T(8,128)(2,1)} async-done(((bf16[6,128,1024]{2,1,0:T(8,128)(2,1)}), bf16[6,128,256]{2,1,0:T(8,128)(2,1)}) %reduce-scatter.2.cloned.1.call-update) | async-done | bytes 393232 | tf_op jit(solution)/shard_map/reduce_scatter | solution.py:45
  40.7 1.2 copy.26
  42.3 10.5 %all_to_all.20 = bf16[2,4,128,256]{3,2,1,0:T(8,128)(2,1)S(1)} all-to-all(bf16[2,4,128,256]{3,2,1,0:T(8,128)(2,1)S(1)} %bitcast.59), channel_id=1, replica_groups=mesh['dp'=4,'half'=2,'own'=4] {'half'}, dimensions={0} | all-to-all | bytes 1048576 | tf_op jit(solution)/shard_map/all_to_all | solution.py:56
  52.8 17.7 %all_to_all.21 = bf16[2,4,128,256]{3,2,0,1:T(8,128)(2,1)S(1)} all-to-all(bf16[2,4,128,256]{3,2,0,1:T(8,128)(2,1)S(1)} %copy.20), channel_id=1, replica_groups=mesh['dp'=4,'half'=2,'own'=4] {'own'}, dimensions={1} | all-to-all | bytes 1048576 | tf_op jit(solution)/shard_map/all_to_all | solution.py:55
  70.6 0.8 copy.21
  71.4 20.2 %all-gather.2.cloned.1.call-done = bf16[1024,1024]{1,0:T(8,128)(2,1)} async-done(((bf16[1024,256]{1,0:T(8,128)(2,1)}), bf16[1024,1024]{1,0:T(8,128)(2,1)}) %all-gather.2.cloned.1.call-update) | async-done | bytes 2097168 | tf_op jit(solution)/shard_map/all_gather | solution.py:69
  91.7 4.2 %fusion.21 = bf16[256,1024]{1,0:T(8,128)(2,1)S(1)} fusion(bf16[1,256,1024]{2,1,0:T(8,128)(2,1)S(1)} %copy-done.1, bf16[1,256,1024]{2,1,0:T(8,128)(2,1)} %param.10, bf16[1,1024,1024]{2,1,0:T(8,128)(2,1)} %param.9, bf16[1024,1024]{1,0:T(8,128)(2,1)} %all-gather.2.cloned.1.call-done, bf16[1,1024,1024]{2,1,0:T(8,128)(2,1)S(1)} %copy-done, s32[]{:T(128)S(6)} %select_n.17), kind=kOutput, calls=%fused_computation.20 | convolution fusion | flops 1077673984 | bytes 6291460 | tf_op jit(solution)/shard_map/dot_general | solution.py:73
  96.2 8.3 %collective-permute-done = bf16[256,1024]{1,0:T(8,128)(2,1)S(1)} collective-permute-done((bf16[256,1024]{1,0:T(8,128)(2,1)S(1)}, bf16[256,1024]{1,0:T(8,128)(2,1)S(1)}, u32[]{:S(2)}, u32[]{:S(2)}) %collective-permute-start) | collective-permute-done | bytes 524320 | tf_op jit(solution)/shard_map/ppermute | solution.py:19
  104.6 1.7 %collective-permute-start.2 = (bf16[256,1024]{1,0:T(8,128)(2,1)S(1)}, bf16[256,1024]{1,0:T(8,128)(2,1)}, u32[]{:S(2)}, u32[]{:S(2)}) collective-permute-start(bf16[256,1024]{1,0:T(8,128)(2,1)S(1)} %fusion.21), channel_id=1, source_target_pairs={{0,24},{8,0},{16,8},{24,16},{1,25},{9,1},{17,9},{25,17},{2,26},{10... | collective-permute-start | bytes 1572872 | tf_op jit(solution)/shard_map/ppermute | solution.py:21
  106.3 11.9 %collective-permute-done.1 = bf16[256,1024]{1,0:T(8,128)(2,1)} collective-permute-done((bf16[256,1024]{1,0:T(8,128)(2,1)S(1)}, bf16[256,1024]{1,0:T(8,128)(2,1)}, u32[]{:S(2)}, u32[]{:S(2)}) %collective-permute-start.1) | collective-permute-done | bytes 524320 | tf_op jit(solution)/shard_map/ppermute | solution.py:19
  118.3 1.9 %constant_dynamic-update-slice_fusion.7 = bf16[2048,1024]{1,0:T(8,128)(2,1)} fusion(bf16[256,1024]{1,0:T(8,128)(2,1)} %collective-permute-done.1), kind=kLoop, calls=%fused_computation.33 | loop fusion | bytes 1048576
  120.1 0.8 constant_dynamic-update-slice_fusion.6
  120.9 0.8 constant_dynamic-update-slice_fusion.5
  121.8 1.9 %constant_dynamic-update-slice_fusion.4 = bf16[2048,1024]{1,0:T(8,128)(2,1)} fusion(bf16[2048,1024]{1,0:T(8,128)(2,1)} %constant_dynamic-update-slice_fusion.5, bf16[256,1024]{1,0:T(8,128)(2,1)} %collective-permute-done.2), kind=kLoop, calls=%fused_computation.30 | loop fusion | bytes 1048576
  123.6 1.9 %constant_dynamic-update-slice_fusion.3 = bf16[2048,1024]{1,0:T(8,128)(2,1)} fusion(bf16[2048,1024]{1,0:T(8,128)(2,1)} %constant_dynamic-update-slice_fusion.4, bf16[256,1024]{1,0:T(8,128)(2,1)} %collective-permute-done.1), kind=kLoop, calls=%fused_computation.29 | loop fusion | bytes 1048576
  125.5 0.8 constant_dynamic-update-slice_fusion.2
  126.3 0.8 constant_dynamic-update-slice_fusion.1
  127.2 1.9 %constant_dynamic-update-slice_fusion = bf16[2048,1024]{1,0:T(8,128)(2,1)} fusion(bf16[2048,1024]{1,0:T(8,128)(2,1)} %constant_dynamic-update-slice_fusion.1, bf16[256,1024]{1,0:T(8,128)(2,1)} %collective-permute-done.2), kind=kLoop, calls=%fused_computation.26 | loop fusion | bytes 1048576 | tf_op jit(solution)/shard_map/jit(_roll_dynamic)/concatenate | solution.py:23
  129.1 4.0 %fusion.12 = bf16[1024,256]{0,1:T(8,128)(2,1)S(1)} fusion(bf16[1,1024,1024]{2,1,0:T(8,128)(2,1)S(1)} %copy-done, bf16[2048,1024]{1,0:T(8,128)(2,1)} %constant_dynamic-update-slice_fusion, s32[]{:T(128)S(6)} %select_n.19, bf16[1,1024,1024]{2,1,0:T(8,128)(2,1)} %param.9, s32[]{:T(128)S(6)} %select_n.17), kind=kOutput, calls=%fused_computation.12 | convolution fusion | flops 1074266112 | bytes 5242888 | tf_op jit(solution)/shard_map/dot_general | solution.py:89
  133.2 9.0 %all_to_all.22 = bf16[2,4,128,256]{3,2,1,0:T(8,128)(2,1)S(1)} all-to-all(bf16[2,4,128,256]{3,2,1,0:T(8,128)(2,1)S(1)} %bitcast.60), channel_id=1, replica_groups=mesh['dp'=4,'half'=2,'own'=4] {'half'}, dimensions={0} | all-to-all | bytes 1048576 | tf_op jit(solution)/shard_map/all_to_all | solution.py:94
  142.3 14.9 %all_to_all.23 = bf16[2,4,128,256]{3,2,0,1:T(8,128)(2,1)S(1)} all-to-all(bf16[2,4,128,256]{3,2,0,1:T(8,128)(2,1)S(1)} %copy.23), channel_id=1, replica_groups=mesh['dp'=4,'half'=2,'own'=4] {'own'}, dimensions={1} | all-to-all | bytes 1048576 | tf_op jit(solution)/shard_map/all_to_all | solution.py:93
  157.8 0.8 copy.31
  (19 shorter events, 2.4 us)
Async XLA Ops:
  6.5 85.1 %copy-start = (bf16[1,1024,1024]{2,1,0:T(8,128)(2,1)S(1)}, bf16[1,1024,1024]{2,1,0:T(8,128)(2,1)}, u32[]{:S(2)}) copy-start(bf16[1,1024,1024]{2,1,0:T(8,128)(2,1)} %param.8) | copy-start | bytes 6291460
  6.5 34.1 %reduce-scatter.2.cloned.1.call-start = ((), (), s32[]{:S(2)}) async-start(), calls=%async_computation.5 | async-start | bytes 1966080 | tf_op jit(solution)/shard_map/reduce_scatter | solution.py:45
  7.3 84.4 %copy-start.1 = (bf16[1,256,1024]{2,1,0:T(8,128)(2,1)S(1)}, bf16[1,256,1024]{2,1,0:T(8,128)(2,1)}, u32[]{:S(2)}) copy-start(bf16[1,256,1024]{2,1,0:T(8,128)(2,1)} %param.11) | copy-start | bytes 1572868
  7.3 84.4 %all-gather.2.cloned.1.call-start = ((), (), s32[]{:S(2)}) async-start(), calls=%async_computation.6 | async-start | bytes 2621440 | tf_op jit(solution)/shard_map/all_gather | solution.py:69
  95.9 8.7 %collective-permute-start = (bf16[256,1024]{1,0:T(8,128)(2,1)S(1)}, bf16[256,1024]{1,0:T(8,128)(2,1)S(1)}, u32[]{:S(2)}, u32[]{:S(2)}) collective-permute-start(bf16[256,1024]{1,0:T(8,128)(2,1)S(1)} %fusion.21), channel_id=1, source_target_pairs={{0,8},{8,16},{16,24},{24,0},{1,9},{9,17},{17,25},{25,1},{2,10},{10... | collective-permute-start | bytes 1572872 | tf_op jit(solution)/shard_map/ppermute | solution.py:19
  104.6 13.7 %collective-permute-start.1 = (bf16[256,1024]{1,0:T(8,128)(2,1)S(1)}, bf16[256,1024]{1,0:T(8,128)(2,1)}, u32[]{:S(2)}, u32[]{:S(2)}) collective-permute-start(bf16[256,1024]{1,0:T(8,128)(2,1)S(1)} %collective-permute-done), channel_id=1, source_target_pairs={{0,8},{8,16},{16,24},{24,0},{1,9},{9,17},{17,25},{25,1},{2,10},{10... | collective-permute-start | bytes 1572872 | tf_op jit(solution)/shard_map/ppermute | solution.py:19
  104.6 17.2 %collective-permute-start.2 = (bf16[256,1024]{1,0:T(8,128)(2,1)S(1)}, bf16[256,1024]{1,0:T(8,128)(2,1)}, u32[]{:S(2)}, u32[]{:S(2)}) collective-permute-start(bf16[256,1024]{1,0:T(8,128)(2,1)S(1)} %fusion.21), channel_id=1, source_target_pairs={{0,24},{8,0},{16,8},{24,16},{1,25},{9,1},{17,9},{25,17},{2,26},{10... | collective-permute-start | bytes 1572872 | tf_op jit(solution)/shard_map/ppermute | solution.py:21
Sparse Core Ops, SparseCore 0:
  9.9 30.7 reduce-scatter.1
  71.6 20.0 all-gather.1
